TPU v7x, 32 devices: a whole 2x2x4 slice. The times are simulated.
32 devices in a mesh: grp: 16 (over z, y, core), seq: 2 (over x).
Axes of the slice: x: 2, y: 2, z: 4, core: 2. Of those that a mesh axis runs over, the one named last changes fastest.
Arguments:
- queries: bfloat16 [8192, 4096], P(('grp', 'seq')), may hold values from -8 to 8
- keys: bfloat16 [8192, 4096], P(('grp', 'seq')), may hold values from -6 to 6
- values: bfloat16 [8192, 4096], P(('grp', 'seq')), may hold values from -6 to 6
- global_pos: int32 [64], P(('grp', 'seq')), may hold values from 0 to 127
- layout: int32 [64, 32], P(('grp', 'seq')), may hold values from 0 to 63, all different within a row
Outputs:
- attended: bfloat16 [8192, 4096], P(('grp', 'seq'))
Inputs may be any that keep to these rules, and one draw needn't show every extreme that they name: `layout`: each row lists 32 different block indices, and every block is listed by some row.
All inputs are finite; a program needn't handle non-finite values.
Results may differ from a plain program's by a relative error of at most 0.0042.
Values may be sent and summed in bfloat16 or wider, within the bound.
A program may use at most 128 MiB of HBM per device.

v0:
```python
import math
import jax
import jax.numpy as jnp
from jax import lax
from jax.sharding import PartitionSpec as P

HEADS = 32
HEAD_DIM = 128
BLOCK = 128


def shifted(value, axis, by):
    count = lax.axis_size(axis)
    pairs = [(i, i + by) for i in range(count) if 0 <= i + by < count]
    return lax.ppermute(value, axis, pairs)


def pooled(source, blocks_dev):
    blocks = source.astype(jnp.float32).reshape(blocks_dev, BLOCK, HEADS, HEAD_DIM).mean(axis=1)
    spread = jnp.mean(blocks * blocks, axis=-1, keepdims=True)
    return (
        (blocks / jnp.sqrt(spread + 1e-06))
        .reshape(blocks_dev, HEADS * HEAD_DIM)
        .astype(jnp.bfloat16)
    )


def shards(queries, keys, values, global_pos, layout):
    rows_dev, model_width = queries.shape
    blocks_dev = rows_dev // BLOCK
    devices = lax.axis_size(("grp", "seq"))
    position = lax.axis_index(("grp", "seq"))
    score_scale = 1.0 / math.sqrt(HEAD_DIM)
    summary_keys = pooled(keys, blocks_dev)
    summary_values = pooled(values, blocks_dev)
    edge_last = jnp.stack([keys[rows_dev - BLOCK :], values[rows_dev - BLOCK :]])
    edge_first = jnp.stack([keys[:BLOCK], values[:BLOCK]])
    from_left = shifted(edge_last, ("grp", "seq"), 1)
    from_right = shifted(edge_first, ("grp", "seq"), -1)
    wide_keys = jnp.concatenate([from_left[0], keys, from_right[0]], axis=0)
    wide_values = jnp.concatenate([from_left[1], values, from_right[1]], axis=0)
    window_keys = jnp.stack(
        [wide_keys[block_at * BLOCK : (block_at + 3) * BLOCK] for block_at in range(blocks_dev)]
    )
    window_values = jnp.stack(
        [wide_values[block_at * BLOCK : (block_at + 3) * BLOCK] for block_at in range(blocks_dev)]
    )
    window_keys = window_keys.reshape(blocks_dev, 3 * BLOCK, HEADS, HEAD_DIM)
    window_values = window_values.reshape(blocks_dev, 3 * BLOCK, HEADS, HEAD_DIM)
    query_blocks = queries.reshape(blocks_dev, BLOCK, HEADS, HEAD_DIM)
    scores = (
        jnp.einsum("bqhd,bkhd->bhqk", query_blocks, window_keys, preferred_element_type=jnp.float32)
        * score_scale
    )
    key_block = (
        position * blocks_dev
        + jnp.arange(blocks_dev, dtype=jnp.int32)[:, None]
        + jnp.arange(3 * BLOCK, dtype=jnp.int32)[None, :] // BLOCK
        - 1
    )
    inside = (key_block >= 0) & (key_block < devices * blocks_dev)
    scores = jnp.where(inside[:, None, None, :], scores, -jnp.inf)
    peak = jnp.max(scores, axis=-1)
    weights = jnp.exp(scores - peak[..., None])
    totals = jnp.sum(weights, axis=-1)
    numerator = jnp.einsum(
        "bhqk,bkhd->bhqd",
        weights.astype(jnp.bfloat16),
        window_values,
        preferred_element_type=jnp.float32,
    )
    is_global = jnp.arange(BLOCK, dtype=jnp.int32)[None, :] == global_pos[:, None]
    group_keys, group_values = (
        lax.all_gather(summary_keys, "seq", axis=0, tiled=True),
        lax.all_gather(summary_values, "seq", axis=0, tiled=True),
    )
    piece_keys = lax.all_gather(group_keys, "grp", axis=0, tiled=True)
    piece_values = lax.all_gather(group_values, "grp", axis=0, tiled=True)
    length = piece_keys.shape[0]
    block_ids = jnp.arange(length, dtype=jnp.int32)
    listed = jnp.any(layout[:, :, None] == block_ids[None, None, :], axis=1)
    visible = listed[:, None, :] | is_global[:, :, None]
    part_scores = (
        jnp.einsum(
            "bqhd,jhd->bhqj",
            query_blocks,
            piece_keys.reshape(length, HEADS, HEAD_DIM),
            preferred_element_type=jnp.float32,
        )
        * score_scale
    )
    part_scores = jnp.where(visible[:, None, :, :], part_scores, -jnp.inf)
    new_peak = jnp.maximum(peak, jnp.max(part_scores, axis=-1))
    factor = jnp.exp(peak - new_peak)
    part_weights = jnp.exp(part_scores - new_peak[..., None])
    totals_next = totals * factor + jnp.sum(part_weights, axis=-1)
    numerator_next = numerator * factor[..., None] + jnp.einsum(
        "bhqj,jhd->bhqd",
        part_weights.astype(jnp.bfloat16),
        piece_values.reshape(length, HEADS, HEAD_DIM),
        preferred_element_type=jnp.float32,
    )
    result = numerator_next / totals_next[..., None]
    return jnp.transpose(result, (0, 2, 1, 3)).reshape(rows_dev, model_width).astype(jnp.bfloat16)


def solution(mesh):
    in_specs = (
        P(("grp", "seq"), None),
        P(("grp", "seq"), None),
        P(("grp", "seq"), None),
        P(("grp", "seq")),
        P(("grp", "seq"), None),
    )
    out_specs = P(("grp", "seq"), None)
    return jax.shard_map(shards, mesh=mesh, in_specs=in_specs, out_specs=out_specs, check_vma=False)
```

profile of v0, /device:TPU:0, one launch (start us, length us, event | category | flops | bytes accessed | tf_op | source)
XLA Modules:
  0.0 201.6 jit_solution(7318982374215686735)
XLA Ops:
  0.0 3.3 %copy.84 = bf16[256,4096]{0,1:T(8,128)(2,1)S(1)} copy(bf16[256,4096]{1,0:T(8,128)(2,1)} %param.6) | data formatting | bytes 4194304 | tf_op args[1]
  3.3 4.1 %copy.85 = bf16[256,4096]{0,1:T(8,128)(2,1)} copy(bf16[256,4096]{1,0:T(8,128)(2,1)} %param.7) | data formatting | bytes 4194304 | tf_op args[2]
  7.4 2.0 slice_bitcast_fusion.2
  9.3 0.0 copy-start
  9.4 1.6 pad_maximum_fusion.1
  10.9 1.3 collective-permute-start.1
  12.2 1.5 pad_maximum_fusion
  13.7 0.0 copy-start.1
  13.7 7.0 %collective-permute-start = (bf16[2,128,4096]{1,2,0:T(8,128)(2,1)}, bf16[2,128,4096]{1,2,0:T(8,128)(2,1)}, u32[]{:S(2)}, u32[]{:S(2)}) collective-permute-start(bf16[2,128,4096]{1,2,0:T(8,128)(2,1)} %pad_maximum_fusion), channel_id=1, source_target_pairs={{0,1},{1,2},{2,3},{3,4},{4,5},{5,6},{6,7},{7,8},{8,9},{9,10},{10,1... | collective-permute-start | bytes 6291464 | tf_op jit(solution)/shard_map/ppermute | solution.py:15
  20.7 0.0 copy-done
  20.7 0.5 convert_bitcast_fusion.1
  21.2 0.0 copy-done.1
  21.2 2.4 %convert_bitcast_fusion = f32[32,8,32,128]{3,1,2,0:T(8,128)} fusion(bf16[256,4096]{1,0:T(8,128)(2,1)S(1)} %copy-done.1), kind=kLoop, calls=%fused_computation.32 | loop fusion | flops 1048576 | bytes 6291456
  23.6 0.8 copy.116
  24.4 0.3 bitcast_reduce_fusion.2
  24.6 0.1 multiply_reduce_fusion.1
  24.7 0.1 divide_convert_fusion.1
  24.9 82.1 %all-gather = bf16[2,2,4096]{2,1,0:T(2,128)(2,1)S(1)} all-gather(bf16[1,2,4096]{2,1,0:T(2,128)(2,1)S(1)} %reshape.201), channel_id=1, replica_groups=mesh['grp'=16,'seq'=2] {'seq'}, dimensions={0}, use_global_device_ids=true | all-gather | bytes 49152 | tf_op jit(solution)/shard_map/all_gather | solution.py:74
  106.9 23.4 %all-gather.1 = bf16[16,4,4096]{2,1,0:T(4,128)(2,1)S(1)} all-gather(bf16[1,4,4096]{2,1,0:T(4,128)(2,1)S(1)} %reshape.203), channel_id=1, replica_groups=mesh['grp'=16,'seq'=2] {'grp'}, dimensions={0}, use_global_device_ids=true | all-gather | bytes 557056 | tf_op jit(solution)/shard_map/all_gather | solution.py:77
  130.3 2.9 %copy.117 = f32[32,8,32,128]{3,2,1,0:T(8,128)S(1)} copy(f32[32,8,32,128]{3,1,2,0:T(8,128)} %convert_bitcast_fusion) | data formatting | bytes 8388608
  133.3 0.3 bitcast_reduce_fusion.1
  133.5 0.1 multiply_reduce_fusion
  133.6 4.1 %copy.96 = bf16[1,256,32,128]{3,1,2,0:T(8,128)(2,1)} copy(bf16[1,256,32,128]{1,3,2,0:T(8,128)(2,1)} %bitcast.75) | data formatting | bytes 4194304 | tf_op jit(solution)/shard_map/concatenate | solution.py:41
  137.7 2.9 %copy.88 = bf16[1,256,32,128]{3,1,2,0:T(8,128)(2,1)} copy(bf16[1,256,32,128]{1,3,2,0:T(8,128)(2,1)S(1)} %bitcast.74) | data formatting | bytes 4194304 | tf_op jit(solution)/shard_map/concatenate | solution.py:40
  140.6 0.0 copy-start.7
  140.6 0.0 copy-start.8
  140.6 2.1 %copy.115 = bf16[32,8,32,128]{3,2,1,0:T(8,128)(2,1)S(1)} copy(bf16[32,8,32,128]{3,1,2,0:T(8,128)(2,1)} %bitcast.83) | data formatting | bytes 4194304
  142.7 0.0 copy-start.3
  142.7 1.5 reshape.193
  144.2 0.1 divide_convert_fusion
  144.3 4.4 %all-gather.2 = bf16[2,2,4096]{2,1,0:T(2,128)(2,1)S(1)} all-gather(bf16[1,2,4096]{2,1,0:T(2,128)(2,1)S(1)} %reshape.205), channel_id=1, replica_groups=mesh['grp'=16,'seq'=2] {'seq'}, dimensions={0}, use_global_device_ids=true | all-gather | bytes 49152 | tf_op jit(solution)/shard_map/all_gather | solution.py:75
  148.8 18.9 %all-gather.3 = bf16[16,4,4096]{2,1,0:T(4,128)(2,1)S(1)} all-gather(bf16[1,4,4096]{2,1,0:T(4,128)(2,1)S(1)} %reshape.207), channel_id=1, replica_groups=mesh['grp'=16,'seq'=2] {'grp'}, dimensions={0}, use_global_device_ids=true | all-gather | bytes 557056 | tf_op jit(solution)/shard_map/all_gather | solution.py:78
  167.7 0.5 reshape.196
  168.2 0.0 copy-done.7
  168.2 0.1 fusion.43
  168.3 0.0 copy-done.8
  168.4 0.1 iota_compare_fusion.1
  168.4 0.1 compare_and_fusion
  168.5 0.1 broadcast_or_fusion
  168.6 3.8 %fusion.54 = (f32[2,32,128]{2,0,1:T(2,128)S(1)}, f32[2,32,128,64]{2,3,0,1:T(8,128)}) fusion(bf16[2,128,32,128]{3,2,1,0:T(8,128)(2,1)S(1)} %bitcast.84, bf16[64,32,128,1]{2,1,0,3:T(8,128)(2,1)} %bitcast.86, pred[2,128,64]{1,2,0:T(8,128)(4,1)S(1)} %broadcast_or_fusion), kind=kOutput, calls=%fused_computation.83 | convolution fusion | flops 135782400 | bytes 4767744 | tf_op jit(solution)/shard_map/bqhd,jhd->bhqj/dot_general | solution.py:84
  172.4 0.0 copy-done.3
  172.4 0.0 collective-permute-done.1
  172.4 1.7 fusion.53
  174.1 1.4 copy.98
  175.5 1.3 copy.92
  176.8 0.0 collective-permute-done
  176.8 1.7 fusion.52
  178.5 1.3 copy.95
  179.8 0.7 copy.87
  180.5 5.2 %bitcast_reduce_fusion = (f32[2,32,128]{2,1,0:T(8,128)S(1)}, f32[2,32,384,128]{3,2,1,0:T(8,128)S(1)}) fusion(pred[2,384]{1,0:T(4,128)(4,1)S(1)} %compare_and_fusion, bf16[2,128,32,128]{3,2,1,0:T(8,128)(2,1)} %bitcast.85, bf16[1,128,32,128]{3,1,2,0:T(8,128)(2,1)} %copy.92, bf16[1,256,32,128]{3,1,2,0:T(8,128)(2,1)} %copy.88, ...), kind=kOutput, calls=%fused_computation.1 | convolution fusion | flops 839901184 | bytes 18907904 | tf_op jit(solution)/shard_map/bqhd,bkhd->bhqk/dot_general | solution.py:52
  185.6 0.0 copy-start.4
  185.6 4.0 %fusion.1 = f32[2,32,128]{2,1,0:T(8,128)S(1)} fusion(f32[2,32,384,128]{3,2,1,0:T(8,128)S(1)} %get-tuple-element.18, f32[2,32,128]{2,1,0:T(8,128)S(1)} %get-tuple-element.17, pred[2,384]{1,0:T(4,128)(4,1)S(1)} %compare_and_fusion), kind=kLoop, calls=%fused_computation.4 | loop fusion | flops 12574720 | bytes 12649216 | tf_op jit(solution)/shard_map/reduce_sum | solution.py:65
  189.7 0.0 copy-done.4
  189.7 0.0 copy-start.2
  189.7 0.0 copy-start.5
  189.7 0.0 copy-start.6
  189.7 0.6 fusion.33
  190.3 0.8 fusion.37
  191.1 0.2 copy-done.2
  191.3 0.3 copy-done.5
  191.5 0.3 copy-done.6
  191.9 6.1 %fusion.25 = bf16[2,128,32,128]{3,1,2,0:T(8,128)(2,1)S(1)} fusion(f32[32,128,2,128]{1,3,0,2:T(8,128)S(1)} %fusion.37, bf16[1,128,32,128]{3,1,2,0:T(8,128)(2,1)S(1)} %copy-done.5, bf16[1,256,32,128]{3,1,2,0:T(8,128)(2,1)S(1)} %copy-done.2, bf16[1,128,32,128]{3,1,2,0:T(8,128)(2,1)S(1)} %copy-done.6, f32[2,32,384,128]{3,2,1,0:T(8,128)S(1)} %get-tuple-element.18, ...), kind=kOutput, calls=%fused_computation.30 | convolution fusion | flops 847249408 | bytes 23167744 | tf_op jit(solution)/shard_map/bhqk,bkhd->bhqd/dot_general | solution.py:66
  197.9 1.4 copy.109
  199.3 2.3 %copy.144 = bf16[32,8,32,128]{3,1,2,0:T(8,128)(2,1)} copy(bf16[32,8,32,128]{3,2,1,0:T(8,128)(2,1)S(1)} %bitcast.78) | data formatting | bytes 4194304
  (11 shorter events, 0.1 us)
Async XLA Ops:
  9.3 11.4 %copy-start = (bf16[256,4096]{1,0:T(8,128)(2,1)S(1)}, bf16[256,4096]{1,0:T(8,128)(2,1)}, u32[]{:S(2)}) copy-start(bf16[256,4096]{1,0:T(8,128)(2,1)} %param.6) | copy-start | bytes 6291460
  10.9 161.5 %collective-permute-start.1 = (bf16[2,128,4096]{1,2,0:T(8,128)(2,1)}, bf16[2,128,4096]{1,2,0:T(8,128)(2,1)}, u32[]{:S(2)}, u32[]{:S(2)}) collective-permute-start(bf16[2,128,4096]{1,2,0:T(8,128)(2,1)} %pad_maximum_fusion.1), channel_id=1, source_target_pairs={{1,0},{2,1},{3,2},{4,3},{5,4},{6,5},{7,6},{8,7},{9,8},{10,9},{11,1... | collective-permute-start | bytes 6291464 | tf_op jit(solution)/shard_map/ppermute | solution.py:15
  13.7 7.5 %copy-start.1 = (bf16[256,4096]{1,0:T(8,128)(2,1)S(1)}, bf16[256,4096]{1,0:T(8,128)(2,1)}, u32[]{:S(2)}) copy-start(bf16[256,4096]{1,0:T(8,128)(2,1)} %param.7) | copy-start | bytes 6291460
  13.7 163.0 %collective-permute-start = (bf16[2,128,4096]{1,2,0:T(8,128)(2,1)}, bf16[2,128,4096]{1,2,0:T(8,128)(2,1)}, u32[]{:S(2)}, u32[]{:S(2)}) collective-permute-start(bf16[2,128,4096]{1,2,0:T(8,128)(2,1)} %pad_maximum_fusion), channel_id=1, source_target_pairs={{0,1},{1,2},{2,3},{3,4},{4,5},{5,6},{6,7},{7,8},{8,9},{9,10},{10,1... | collective-permute-start | bytes 6291464 | tf_op jit(solution)/shard_map/ppermute | solution.py:15
  140.6 27.6 %copy-start.7 = (s32[2,32]{1,0:T(2,128)S(1)}, s32[2,32]{1,0:T(2,128)}, u32[]{:S(2)}) copy-start(s32[2,32]{1,0:T(2,128)} %param.9) | copy-start | bytes 772
  140.6 27.7 %copy-start.8 = (s32[2]{0:T(128)S(1)}, s32[2]{0:T(128)}, u32[]{:S(2)}) copy-start(s32[2]{0:T(128)} %param.8) | copy-start | bytes 28
  142.7 29.7 %copy-start.3 = (bf16[32,8,32,128]{3,2,1,0:T(8,128)(2,1)}, bf16[32,8,32,128]{3,2,1,0:T(8,128)(2,1)S(1)}, u32[]{:S(2)}) copy-start(bf16[32,8,32,128]{3,2,1,0:T(8,128)(2,1)S(1)} %copy.115) | copy-start | bytes 6291460
  185.6 4.1 %copy-start.4 = (f32[2,32,128,64]{2,3,0,1:T(8,128)S(1)}, f32[2,32,128,64]{2,3,0,1:T(8,128)}, u32[]{:S(2)}) copy-start(f32[2,32,128,64]{2,3,0,1:T(8,128)} %get-tuple-element.20) | copy-start | bytes 6291460
  189.7 1.6 copy-start.2
  189.7 1.8 copy-start.5
  189.7 2.2 %copy-start.6 = (bf16[1,128,32,128]{3,1,2,0:T(8,128)(2,1)S(1)}, bf16[1,128,32,128]{3,1,2,0:T(8,128)(2,1)}, u32[]{:S(2)}) copy-start(bf16[1,128,32,128]{3,1,2,0:T(8,128)(2,1)} %copy.95) | copy-start | bytes 3145732
where the time goes:
time: 202 us
  blocking collectives  129 us (64%)
  local copies, waits for them, and re-layouts  36.7 us (18%)
  matrix products  15.8 us (8%)
  other arithmetic  11.8 us (6%)
  starting transfers between devices  8.25 us (4%)
    all_gather x1, blocking collectives, shards(): lax.all_gather(summary_keys, 'seq', axis=0, tiled=True)  82.1 us
    all_gather x1, blocking collectives, shards(): piece_keys = lax.all_gather(group_keys, 'grp', axis=0, tiled=True)  23.4 us
    all_gather x1, blocking collectives, shards(): piece_values = lax.all_gather(group_values, 'grp', axis=0, tiled=True)  18.9 us
    unnamed x28, local copies, waits for them, and re-layouts  16.3 us
    ppermute x2, starting transfers between devices, shifted(): return lax.ppermute(value, axis, pairs)  8.25 us
    concatenate x3, local copies, waits for them, and re-layouts, shards(): wide_values = jnp.concatenate([from_left[1], values, from_right[1]], axis=0)  6.82 us
    dot_general x1, matrix products, shards(): jnp.einsum('bhqk,bkhd->bhqd', weights.astype(jnp.bfloat16), window_values...  6.06 us
    dot_general x1, matrix products, shards(): jnp.einsum('bqhd,bkhd->bhqk', query_blocks, window_keys, preferred_elemen...  5.16 us
  transfers between devices with their start and end apart: 2, of which 0 were waited for; matrix products, arithmetic and copies ran while one was open for 14% of the time, Pallas kernels for 0%

commit v1 on v0

--- a/solution.py
+++ b/solution.py
@@ -74,8 +74,13 @@
         lax.all_gather(summary_keys, "seq", axis=0, tiled=True),
         lax.all_gather(summary_values, "seq", axis=0, tiled=True),
     )
-    piece_keys = lax.all_gather(group_keys, "grp", axis=0, tiled=True)
-    piece_values = lax.all_gather(group_values, "grp", axis=0, tiled=True)
+    piece_keys, piece_values = jnp.split(
+        jax.lax.all_gather(
+            jnp.concatenate([group_keys, group_values], axis=1), "grp", axis=0, tiled=True
+        ),
+        [group_keys.shape[1]],
+        1,
+    )
     length = piece_keys.shape[0]
     block_ids = jnp.arange(length, dtype=jnp.int32)
     listed = jnp.any(layout[:, :, None] == block_ids[None, None, :], axis=1)

time: 202 us -> 159 us (0.79)
  the two profiles are of different devices: /device:TPU:0 before, /device:TPU:1 now
where the time goes in v1:
time: 159 us; the launch traced here: 158 us
  waiting for transfers between devices  68.9 us (43%)
  local copies, waits for them, and re-layouts  33.9 us (21%)
  matrix products  14.5 us (9%)
  between operations  13.7 us (9%)
  other arithmetic  12 us (8%)
  starting transfers between devices  8.16 us (5%)
  blocking collectives  7.19 us (5%)
    ppermute x2, waiting for transfers between devices, shifted(): return lax.ppermute(value, axis, pairs)  47.7 us
    all_gather x1, waiting for transfers between devices, shards(): jax.lax.all_gather(jnp.concatenate([group_keys, group_values], axis=1), '...  21.2 us
    unnamed x29, local copies, waits for them, and re-layouts  16.2 us
    ppermute x2, starting transfers between devices, shifted(): return lax.ppermute(value, axis, pairs)  8.16 us
    concatenate x3, local copies, waits for them, and re-layouts, shards(): wide_values = jnp.concatenate([from_left[1], values, from_right[1]], axis=0)  6.11 us
    dot_general x1, matrix products, shards(): jnp.einsum('bhqk,bkhd->bhqd', weights.astype(jnp.bfloat16), window_values...  6.06 us
    dot_general x1, matrix products, shards(): jnp.einsum('bqhd,bkhd->bhqk', query_blocks, window_keys, preferred_elemen...  4.9 us
    concatenate x3, local copies, waits for them, and re-layouts, shards(): wide_keys = jnp.concatenate([from_left[0], keys, from_right[0]], axis=0)  4.86 us
  transfers between devices with their start and end apart: 3, of which 3 were waited for; matrix products, arithmetic and copies ran while one was open for 19% of the time, Pallas kernels for 0%

profile of v1, /device:TPU:1, one launch (start us, length us, event | category | flops | bytes accessed | tf_op | source)
XLA Modules:
  0.0 158.4 jit_solution(4857567678383922906)
XLA Ops:
  6.5 0.0 all-gather.5.cloned.1.call-start
  6.5 2.1 %convert_bitcast_fusion.1 = f32[32,8,32,128]{3,1,2,0:T(8,128)S(1)} fusion(bf16[256,4096]{1,0:T(8,128)(2,1)} %param.6), kind=kLoop, calls=%fused_computation.33 | loop fusion | flops 1048576 | bytes 6291456
  8.6 0.8 copy.117
  9.4 0.0 copy-start
  9.4 0.3 bitcast_reduce_fusion.2
  9.7 0.1 multiply_reduce_fusion.1
  9.8 0.1 divide_convert_fusion.1
  9.9 3.9 %all-gather = bf16[2,2,4096]{2,1,0:T(2,128)(2,1)S(1)} all-gather(bf16[1,2,4096]{2,1,0:T(2,128)(2,1)S(1)} %reshape.201), channel_id=1, replica_groups=mesh['grp'=16,'seq'=2] {'seq'}, dimensions={0}, use_global_device_ids=true | all-gather | bytes 49152 | tf_op jit(solution)/shard_map/all_gather | solution.py:74
  13.8 0.0 copy-done
  13.8 0.5 convert_bitcast_fusion
  14.3 0.8 copy.118
  15.1 0.3 bitcast_reduce_fusion.1
  15.4 0.1 multiply_reduce_fusion
  15.5 0.1 divide_convert_fusion
  15.6 3.3 %all-gather.1 = bf16[2,2,4096]{2,1,0:T(2,128)(2,1)S(1)} all-gather(bf16[1,2,4096]{2,1,0:T(2,128)(2,1)S(1)} %reshape.203), channel_id=1, replica_groups=mesh['grp'=16,'seq'=2] {'seq'}, dimensions={0}, use_global_device_ids=true | all-gather | bytes 49152 | tf_op jit(solution)/shard_map/all_gather | solution.py:75
  18.8 0.7 maximum_bitcast_fusion
  19.5 0.0 all-gather.5.cloned.1.call-update
  19.5 3.3 %copy.84 = bf16[256,4096]{0,1:T(8,128)(2,1)S(1)} copy(bf16[256,4096]{1,0:T(8,128)(2,1)} %param.6) | data formatting | bytes 4194304 | tf_op args[1]
  22.8 4.1 %copy.85 = bf16[256,4096]{0,1:T(8,128)(2,1)} copy(bf16[256,4096]{1,0:T(8,128)(2,1)} %param.7) | data formatting | bytes 4194304 | tf_op args[2]
  26.9 2.0 %slice_bitcast_fusion.2 = (bf16[1,128,4096]{1,2,0:T(8,128)(2,1)S(1)}, bf16[1,128,4096]{1,2,0:T(8,128)(2,1)S(1)}, bf16[1,128,4096]{1,2,0:T(8,128)(2,1)S(1)}, bf16[1,128,4096]{1,2,0:T(8,128)(2,1)S(1)}) fusion(bf16[256,4096]{0,1:T(8,128)(2,1)} %copy.85, bf16[256,4096]{0,1:T(8,128)(2,1)S(1)} %copy.84), kind=kLoop, calls=%fused_computation.46 | loop fusion | bytes 8388608 | tf_op jit(solution)/shard_map/stack | solution.py:36
  28.9 1.5 pad_maximum_fusion.1
  30.4 6.3 %collective-permute-start.1 = (bf16[2,128,4096]{1,2,0:T(8,128)(2,1)}, bf16[2,128,4096]{1,2,0:T(8,128)(2,1)}, u32[]{:S(2)}, u32[]{:S(2)}) collective-permute-start(bf16[2,128,4096]{1,2,0:T(8,128)(2,1)} %pad_maximum_fusion.1), channel_id=1, source_target_pairs={{1,0},{2,1},{3,2},{4,3},{5,4},{6,5},{7,6},{8,7},{9,8},{10,9},{11,1... | collective-permute-start | bytes 6291464 | tf_op jit(solution)/shard_map/ppermute | solution.py:15
  36.6 1.5 pad_maximum_fusion
  38.1 1.9 %collective-permute-start = (bf16[2,128,4096]{1,2,0:T(8,128)(2,1)}, bf16[2,128,4096]{1,2,0:T(8,128)(2,1)}, u32[]{:S(2)}, u32[]{:S(2)}) collective-permute-start(bf16[2,128,4096]{1,2,0:T(8,128)(2,1)} %pad_maximum_fusion), channel_id=1, source_target_pairs={{0,1},{1,2},{2,3},{3,4},{4,5},{5,6},{6,7},{7,8},{8,9},{9,10},{10,1... | collective-permute-start | bytes 6291464 | tf_op jit(solution)/shard_map/ppermute | solution.py:15
  40.1 4.1 %copy.96 = bf16[1,256,32,128]{3,1,2,0:T(8,128)(2,1)} copy(bf16[1,256,32,128]{1,3,2,0:T(8,128)(2,1)} %bitcast.86) | data formatting | bytes 4194304 | tf_op jit(solution)/shard_map/concatenate | solution.py:41
  44.2 0.0 copy-start.6
  44.2 2.9 %copy.88 = bf16[1,256,32,128]{3,1,2,0:T(8,128)(2,1)} copy(bf16[1,256,32,128]{1,3,2,0:T(8,128)(2,1)S(1)} %bitcast.85) | data formatting | bytes 4194304 | tf_op jit(solution)/shard_map/concatenate | solution.py:40
  47.0 2.2 %copy.116 = bf16[32,8,32,128]{3,2,1,0:T(8,128)(2,1)S(1)} copy(bf16[32,8,32,128]{3,1,2,0:T(8,128)(2,1)} %bitcast.94) | data formatting | bytes 4194304
  49.2 0.0 copy-start.2
  49.3 0.0 copy-done.6
  49.3 0.1 fusion.42
  49.4 0.0 copy-done.7
  49.4 0.1 iota_compare_fusion.1
  49.5 0.1 compare_and_fusion
  49.5 0.1 broadcast_or_fusion
  49.6 21.2 %all-gather.5.cloned.1.call-done = bf16[16,4,8192]{2,1,0:T(4,128)(2,1)} async-done(((bf16[1,4,8192]{2,1,0:T(4,128)(2,1)}), bf16[16,4,8192]{2,1,0:T(4,128)(2,1)}) %all-gather.5.cloned.1.call-update) | async-done | bytes 1048592 | tf_op jit(solution)/shard_map/all_gather | solution.py:78
  70.9 1.3 reshape.206
  72.2 0.9 slice_bitcast_fusion.4
  73.1 0.1 copy.119
  73.2 2.8 %fusion.53 = (f32[2,32,128]{2,0,1:T(2,128)S(1)}, f32[2,32,128,64]{2,3,0,1:T(8,128)}) fusion(bf16[2,128,32,128]{3,2,1,0:T(8,128)(2,1)S(1)} %bitcast.95, bf16[64,32,128,1]{2,1,0,3:T(8,128)(2,1)S(1)} %bitcast.97, pred[2,128,64]{1,2,0:T(8,128)(4,1)S(1)} %broadcast_or_fusion), kind=kOutput, calls=%fused_computation.86 | convolution fusion | flops 135782400 | bytes 4767744 | tf_op jit(solution)/shard_map/bqhd,jhd->bhqj/dot_general | solution.py:89
  75.9 0.0 copy-done.2
  76.0 28.0 %collective-permute-done.1 = bf16[2,128,4096]{1,2,0:T(8,128)(2,1)} collective-permute-done((bf16[2,128,4096]{1,2,0:T(8,128)(2,1)}, bf16[2,128,4096]{1,2,0:T(8,128)(2,1)}, u32[]{:S(2)}, u32[]{:S(2)}) %collective-permute-start.1) | collective-permute-done | bytes 2097184 | tf_op jit(solution)/shard_map/ppermute | solution.py:15
  104.0 1.7 %fusion.52 = (bf16[1,128,4096]{1,2,0:T(8,128)(2,1)S(1)}, bf16[1,128,4096]{1,2,0:T(8,128)(2,1)S(1)}) fusion(bf16[2,128,4096]{1,2,0:T(8,128)(2,1)} %collective-permute-done.1), kind=kLoop, calls=%fused_computation.85 | loop fusion | bytes 4194304 | tf_op jit(solution)/shard_map/slice | solution.py:41
  105.7 0.7 copy.98
  106.3 1.3 copy.92
  107.7 19.6 %collective-permute-done = bf16[2,128,4096]{1,2,0:T(8,128)(2,1)} collective-permute-done((bf16[2,128,4096]{1,2,0:T(8,128)(2,1)}, bf16[2,128,4096]{1,2,0:T(8,128)(2,1)}, u32[]{:S(2)}, u32[]{:S(2)}) %collective-permute-start) | collective-permute-done | bytes 2097184 | tf_op jit(solution)/shard_map/ppermute | solution.py:15
  127.3 1.7 %fusion.51 = (bf16[1,128,4096]{1,2,0:T(8,128)(2,1)S(1)}, bf16[1,128,4096]{1,2,0:T(8,128)(2,1)S(1)}) fusion(bf16[2,128,4096]{1,2,0:T(8,128)(2,1)} %collective-permute-done), kind=kLoop, calls=%fused_computation.84 | loop fusion | bytes 4194304 | tf_op jit(solution)/shard_map/slice | solution.py:41
  129.0 1.3 copy.95
  130.3 0.7 copy.87
  131.0 4.9 %bitcast_reduce_fusion = (f32[2,32,128]{2,1,0:T(8,128)S(1)}, f32[2,32,384,128]{3,2,1,0:T(8,128)S(1)}) fusion(pred[2,384]{1,0:T(4,128)(4,1)S(1)} %compare_and_fusion, bf16[2,128,32,128]{3,2,1,0:T(8,128)(2,1)} %bitcast.96, bf16[1,128,32,128]{3,1,2,0:T(8,128)(2,1)} %copy.92, bf16[1,256,32,128]{3,1,2,0:T(8,128)(2,1)} %copy.88, ...), kind=kOutput, calls=%fused_computation.1 | convolution fusion | flops 839901184 | bytes 18907904 | tf_op jit(solution)/shard_map/bqhd,bkhd->bhqk/dot_general | solution.py:52
  135.9 0.0 copy-start.3
  135.9 0.0 copy-start.4
  135.9 3.9 %fusion.1 = f32[2,32,128]{2,1,0:T(8,128)S(1)} fusion(f32[2,32,384,128]{3,2,1,0:T(8,128)S(1)} %get-tuple-element.20, f32[2,32,128]{2,1,0:T(8,128)S(1)} %get-tuple-element.19, pred[2,384]{1,0:T(4,128)(4,1)S(1)} %compare_and_fusion), kind=kLoop, calls=%fused_computation.4 | loop fusion | flops 12574720 | bytes 12649216 | tf_op jit(solution)/shard_map/reduce_sum | solution.py:65
  139.9 0.0 copy-done.3
  139.9 0.0 copy-start.1
  139.9 0.0 copy-start.5
  139.9 0.6 fusion.33
  140.6 0.0 copy-done.4
  140.6 0.8 fusion.37
  141.3 0.2 copy-done.1
  141.5 0.3 copy-done.5
  141.8 6.1 %fusion.25 = bf16[2,128,32,128]{3,1,2,0:T(8,128)(2,1)S(1)} fusion(f32[32,128,2,128]{1,3,0,2:T(8,128)S(1)} %fusion.37, bf16[1,128,32,128]{3,1,2,0:T(8,128)(2,1)S(1)} %copy.98, bf16[1,256,32,128]{3,1,2,0:T(8,128)(2,1)S(1)} %copy-done.1, bf16[1,128,32,128]{3,1,2,0:T(8,128)(2,1)S(1)} %copy-done.5, f32[2,32,384,128]{3,2,1,0:T(8,128)S(1)} %get-tuple-element.20, ...), kind=kOutput, calls=%fused_computation.30 | convolution fusion | flops 847249408 | bytes 23167744 | tf_op jit(solution)/shard_map/bhqk,bkhd->bhqd/dot_general | solution.py:66
  147.8 1.4 copy.109
  149.2 2.3 %copy.146 = bf16[32,8,32,128]{3,1,2,0:T(8,128)(2,1)} copy(bf16[32,8,32,128]{3,2,1,0:T(8,128)(2,1)S(1)} %bitcast.89) | data formatting | bytes 4194304
  (12 shorter events, 0.1 us)
Async XLA Ops:
  6.5 64.3 %all-gather.5.cloned.1.call-start = ((), (), s32[]{:S(2)}) async-start(), calls=%async_computation | async-start | bytes 1114112 | tf_op jit(solution)/shard_map/all_gather | solution.py:78
  9.4 4.5 %copy-start = (bf16[256,4096]{1,0:T(8,128)(2,1)S(1)}, bf16[256,4096]{1,0:T(8,128)(2,1)}, u32[]{:S(2)}) copy-start(bf16[256,4096]{1,0:T(8,128)(2,1)} %param.7) | copy-start | bytes 6291460
  30.4 73.6 %collective-permute-start.1 = (bf16[2,128,4096]{1,2,0:T(8,128)(2,1)}, bf16[2,128,4096]{1,2,0:T(8,128)(2,1)}, u32[]{:S(2)}, u32[]{:S(2)}) collective-permute-start(bf16[2,128,4096]{1,2,0:T(8,128)(2,1)} %pad_maximum_fusion.1), channel_id=1, source_target_pairs={{1,0},{2,1},{3,2},{4,3},{5,4},{6,5},{7,6},{8,7},{9,8},{10,9},{11,1... | collective-permute-start | bytes 6291464 | tf_op jit(solution)/shard_map/ppermute | solution.py:15
  38.1 89.2 %collective-permute-start = (bf16[2,128,4096]{1,2,0:T(8,128)(2,1)}, bf16[2,128,4096]{1,2,0:T(8,128)(2,1)}, u32[]{:S(2)}, u32[]{:S(2)}) collective-permute-start(bf16[2,128,4096]{1,2,0:T(8,128)(2,1)} %pad_maximum_fusion), channel_id=1, source_target_pairs={{0,1},{1,2},{2,3},{3,4},{4,5},{5,6},{6,7},{7,8},{8,9},{9,10},{10,1... | collective-permute-start | bytes 6291464 | tf_op jit(solution)/shard_map/ppermute | solution.py:15
  44.2 5.1 %copy-start.6 = (s32[2,32]{1,0:T(2,128)S(1)}, s32[2,32]{1,0:T(2,128)}, u32[]{:S(2)}) copy-start(s32[2,32]{1,0:T(2,128)} %param.9) | copy-start | bytes 772
  44.2 5.2 %copy-start.7 = (s32[2]{0:T(128)S(1)}, s32[2]{0:T(128)}, u32[]{:S(2)}) copy-start(s32[2]{0:T(128)} %param.8) | copy-start | bytes 28
  49.2 26.7 %copy-start.2 = (bf16[32,8,32,128]{3,2,1,0:T(8,128)(2,1)}, bf16[32,8,32,128]{3,2,1,0:T(8,128)(2,1)S(1)}, u32[]{:S(2)}) copy-start(bf16[32,8,32,128]{3,2,1,0:T(8,128)(2,1)S(1)} %copy.116) | copy-start | bytes 6291460
  135.9 4.0 %copy-start.3 = (f32[2,32,128,64]{2,3,0,1:T(8,128)S(1)}, f32[2,32,128,64]{2,3,0,1:T(8,128)}, u32[]{:S(2)}) copy-start(f32[2,32,128,64]{2,3,0,1:T(8,128)} %get-tuple-element.22) | copy-start | bytes 6291460
  135.9 4.6 %copy-start.4 = (bf16[8,32,8,128]{3,2,1,0:T(8,128)(2,1)S(1)}, bf16[8,32,8,128]{3,2,1,0:T(8,128)(2,1)}, u32[]{:S(2)}) copy-start(bf16[8,32,8,128]{3,2,1,0:T(8,128)(2,1)} %get-tuple-element.17) | copy-start | bytes 1572868
  139.9 1.6 %copy-start.1 = (bf16[1,256,32,128]{3,1,2,0:T(8,128)(2,1)S(1)}, bf16[1,256,32,128]{3,1,2,0:T(8,128)(2,1)}, u32[]{:S(2)}) copy-start(bf16[1,256,32,128]{3,1,2,0:T(8,128)(2,1)} %copy.96) | copy-start | bytes 6291460
  139.9 1.8 %copy-start.5 = (bf16[1,128,32,128]{3,1,2,0:T(8,128)(2,1)S(1)}, bf16[1,128,32,128]{3,1,2,0:T(8,128)(2,1)}, u32[]{:S(2)}) copy-start(bf16[1,128,32,128]{3,1,2,0:T(8,128)(2,1)} %copy.95) | copy-start | bytes 3145732
Sparse Core Ops, SparseCore 0:
  19.6 51.1 all-gather.4
